TPU v7x, 32 devices: a whole 2x2x4 slice. The times are simulated.
32 devices in a mesh: img: 8 (over y, x, core), strip: 4 (over z).
Axes of the slice: x: 2, y: 2, z: 4, core: 2. Of those that a mesh axis runs over, the one named last changes fastest.
Arguments:
- image_in: bfloat16 [8, 128, 128, 128], P('img', 'strip'), may hold values from -6 to 6
- cotangent: bfloat16 [8, 128, 128, 128], P('img', 'strip'), may hold values from -6 to 6
- conv1_w: bfloat16 [3, 3, 128, 128], replicated, may hold values from -0.1875 to 0.1875
- conv2_w: bfloat16 [3, 3, 128, 128], replicated, may hold values from -0.1875 to 0.1875
- norm1_gain: float32 [128], replicated, may hold values from 0.5 to 1.5
- norm1_shift: float32 [128], replicated, may hold values from -3 to 3
- norm2_gain: float32 [128], replicated, may hold values from 0.5 to 1.5
- norm2_shift: float32 [128], replicated, may hold values from -3 to 3
- strip_rows: int32 [8, 4], P('img', 'strip'), may hold values from 1 to 32, 64 in all within a row
Outputs:
- image_grad: bfloat16 [8, 128, 128, 128], P('img', 'strip')
- conv1_grad: float32 [1152, 128], P('img')
- conv2_grad: float32 [1152, 128], P('img')
- norm_grads: float32 [4, 128], replicated
Inputs may be any that keep to these rules, and one draw needn't show every extreme that they name: `strip_rows`: each image's 4 strip lengths sum to 64; in every image one strip holds exactly 32 rows.
All inputs are finite; a program needn't handle non-finite values. No bound on the sum of `strip_rows` on one device may be relied on, other than what follows from the above.
Results may differ from a plain program's by a relative error of at most 0.0055.
Values may be sent and summed in bfloat16 or wider, within the bound.
A program may use at most 64 MiB of HBM per device.

v0:
```python
import functools

import jax
import jax.numpy as jnp
from jax import lax
from jax.experimental import pallas as pl
from jax.experimental.pallas import tpu as pltpu
from jax.sharding import PartitionSpec as P

GROUPS = 32
EPSILON = 1e-06
F32 = jnp.float32
BF16 = jnp.bfloat16
MESH = pl.DeviceIdType.MESH


def ceil_to(value, unit):
    return -(-value // unit) * unit


def sigmoid(z):
    return 0.5 * jnp.tanh(0.5 * z) + 0.5


def group_sum(block, size):
    lanes = block.shape[1]
    lane = lax.broadcasted_iota(jnp.int32, block.shape, 1)
    step = 1
    while step < size:
        upper = pltpu.roll(block, lanes - step, 1)
        lower = pltpu.roll(block, step, 1)
        block = block + jnp.where((lane & step) == 0, upper, lower)
        step *= 2
    return block


def fold(values):
    return jnp.sum(values.reshape(values.shape[0] // 8, 8, values.shape[1]), axis=0)


def flat(block):
    return jnp.broadcast_to(jnp.sum(block, axis=0, keepdims=True), block.shape)


def by_row(parts):
    row = lax.broadcasted_iota(jnp.int32, parts[0].shape, 0)
    out = jnp.zeros_like(parts[0])
    for k, part in enumerate(parts):
        out = jnp.where(row == k, part, out)
    return out


def kernel(
    n,
    m,
    rows_out,
    quota,
    len_ref,
    x_ref,
    g_ref,
    w1_ref,
    w2_ref,
    gain1_ref,
    shift1_ref,
    gain2_ref,
    shift2_ref,
    out_ref,
    grad1_ref,
    grad2_ref,
    norm_ref,
    buf1,
    buf2,
    bufd,
    hidden,
    back,
    act2,
    dh,
    gt,
    wp,
    acc,
    full,
    edge,
    halo,
    xbuf,
    nbuf,
    rs,
    got1,
    part,
    got2,
    ag,
    halo_send,
    halo_recv,
    x_send,
    x_recv,
    n_send,
    n_recv,
    s1_send,
    s1_recv,
    s2_send,
    s2_recv,
    s3_send,
    s3_recv,
):
    _, slots, cols, chans = x_ref.shape
    size = chans // GROUPS
    me = lax.axis_index("strip")
    img = lax.axis_index("img")
    length = len_ref[0, 0]
    last = jnp.maximum(length - 1, 0)
    height = slots * n // 2
    cells = float(height * cols * size)

    barrier = pltpu.get_barrier_semaphore()
    for d in range(1, n):
        pl.semaphore_signal(
            barrier, inc=1, device_id={"strip": lax.rem(me + d, n)}, device_id_type=MESH
        )
    for d in range(1, m):
        pl.semaphore_signal(
            barrier, inc=1, device_id={"img": lax.rem(img + d, m)}, device_id_type=MESH
        )

    def send_halo(kind, first, last):
        below = pltpu.make_async_remote_copy(
            src_ref=last,
            dst_ref=halo.at[kind, 0],
            send_sem=halo_send.at[kind, 0],
            recv_sem=halo_recv.at[kind, 0],
            device_id={"strip": lax.rem(me + 1, n)},
            device_id_type=MESH,
        )
        above = pltpu.make_async_remote_copy(
            src_ref=first,
            dst_ref=halo.at[kind, 1],
            send_sem=halo_send.at[kind, 1],
            recv_sem=halo_recv.at[kind, 1],
            device_id={"strip": lax.rem(me + n - 1, n)},
            device_id_type=MESH,
        )
        below.start()
        above.start()
        return [below, above]

    def send_block(kind, block):
        xbuf[kind, me] = block
        copies = []
        for d in range(1, n):
            copy = pltpu.make_async_remote_copy(
                src_ref=xbuf.at[kind, me],
                dst_ref=xbuf.at[kind, me],
                send_sem=x_send.at[kind, d - 1],
                recv_sem=x_recv.at[kind, d - 1],
                device_id={"strip": lax.rem(me + d, n)},
                device_id_type=MESH,
            )
            copy.start()
            copies.append(copy)
        return copies

    def wait_all(copies):
        for copy in copies:
            copy.wait()

    def live(row):
        return jnp.full((cols, chans), row, jnp.int32) < length

    zero8 = jnp.zeros((8, chans), F32)

    def local_stats(load):
        def add(r, total):
            return total + fold(jnp.where(live(r), load(r), 0.0))

        total = lax.fori_loop(0, slots, add, zero8, unroll=2)
        count = (jnp.full((8, chans), length, jnp.int32) * (cols * size)).astype(F32)
        mean = group_sum(flat(total), size) / count
        one = mean[0:1]

        def spread(r, total):
            centered = jnp.where(live(r), load(r) - one, 0.0)
            return total + fold(centered * centered)

        spread_sum = lax.fori_loop(0, slots, spread, zero8, unroll=2)
        return by_row([count, mean, group_sum(flat(spread_sum), size)])

    def joined_stats(kind):
        count = xbuf[kind, 0, 0:1]
        weighted = count * xbuf[kind, 0, 1:2]
        total = count
        for k in range(1, n):
            count = xbuf[kind, k, 0:1]
            total = total + count
            weighted = weighted + count * xbuf[kind, k, 1:2]
        mean = weighted / total
        spread = jnp.zeros_like(mean)
        for k in range(n):
            delta = xbuf[kind, k, 1:2] - mean
            spread = spread + (xbuf[kind, k, 2:3] + xbuf[kind, k, 0:1] * delta * delta)
        return mean, lax.rsqrt(spread / cells + EPSILON)

    def joined_sums(kind):
        total = xbuf[kind, 0]
        for k in range(1, n):
            total = total + xbuf[kind, k]
        return total

    def means_of(sums, gain):
        both = group_sum(sums * gain, size) / cells
        return both[0:1], both[1:2]

    column = lax.broadcasted_iota(jnp.int32, (cols, chans), 0)
    has_above = jnp.where(me > 0, 1, 0)
    has_below = jnp.where(me < n - 1, 1, 0)

    def build(buf, kind, load, change):
        def one_row(i, carry):
            r = i - 1
            own = load(jnp.clip(r, 0, slots - 1)).astype(F32)
            at = jnp.full((cols, chans), r, jnp.int32)
            value = jnp.where(at < 0, halo[kind, 0].astype(F32), own)
            value = jnp.where(at == length, halo[kind, 1].astype(F32), value)
            keep = jnp.where(at < 0, has_above, jnp.where(at == length, has_below, 1))
            keep = jnp.where(at > length, 0, keep)
            value = jnp.where(keep > 0, change(value), 0.0)
            before = jnp.where(column == 0, 0.0, pltpu.roll(value, 1, 0))
            after = jnp.where(column == cols - 1, 0.0, pltpu.roll(value, cols - 1, 0))
            buf[i, :, 0:chans] = before.astype(BF16)
            buf[i, :, chans : 2 * chans] = value.astype(BF16)
            buf[i, :, 2 * chans : 3 * chans] = after.astype(BF16)
            return carry

        lax.fori_loop(0, slots + 2, one_row, 0, unroll=2)
        buf[slots + 2] = jnp.zeros((cols, 3 * chans), BF16)
        buf[slots + 3] = jnp.zeros((cols, 3 * chans), BF16)

    def load_forward(w_ref):
        for j in range(4):
            for b in range(3):
                at = (j * 3 + b) * chans
                for t in range(2):
                    a = j - t
                    tap = w_ref[a, b] if 0 <= a <= 2 else jnp.zeros((chans, chans), BF16)
                    wp[at : at + chans, t * chans : (t + 1) * chans] = tap

    def load_backward(w_ref):
        for j in range(4):
            for b in range(3):
                at = (j * 3 + b) * chans
                for t in range(2):
                    a = j - t
                    if 0 <= a <= 2:
                        tap = w_ref[2 - a, 2 - b].astype(F32).T.astype(BF16)
                    else:
                        tap = jnp.zeros((chans, chans), BF16)
                    wp[at : at + chans, t * chans : (t + 1) * chans] = tap

    pairs = 4

    def convolve(buf, out):
        def step(q, carry):
            base = q * (2 * pairs)
            pieces = []
            for p in range(pairs):
                pieces.append(
                    jnp.concatenate([buf[base + (2 * p + j)] for j in range(4)], axis=1)
                )
            result = jnp.dot(
                jnp.concatenate(pieces, axis=0), wp[...], preferred_element_type=F32
            )
            for p in range(pairs):
                for t in range(2):
                    out[base + (2 * p + t)] = result[
                        p * cols : (p + 1) * cols, t * chans : (t + 1) * chans
                    ]
            return carry

        lax.fori_loop(0, slots // (2 * pairs), step, 0)

    def kernel_grad(buf):
        acc[...] = jnp.zeros_like(acc)
        rows = 4

        def step(q, carry):
            left = jnp.concatenate(
                [
                    jnp.concatenate([gt[q * rows + (k + 2 - a)] for k in range(rows)], axis=1)
                    for a in range(3)
                ],
                axis=0,
            )
            right = jnp.concatenate([buf[q * rows + k] for k in range(rows)], axis=0)
            acc[...] += jnp.dot(left, right, preferred_element_type=F32)
            return carry

        lax.fori_loop(0, (slots + 4) // rows, step, 0)
        for a in range(3):
            for b in range(3):
                at = (a * 3 + b) * chans
                full[at : at + chans] = acc[
                    a * chans : (a + 1) * chans, b * chans : (b + 1) * chans
                ].T

    def scatter_strips(k):
        for i in range(m):
            for s in range(n):
                low = min(s * quota, rows_out)
                high = min(low + quota, rows_out)
                if high > low:
                    rs[k, i, s, 0 : high - low] = full[i * rows_out + low : i * rows_out + high]
                if high - low < quota:
                    rs[k, i, s, high - low : quota] = jnp.zeros(
                        (quota - (high - low), chans), F32
                    )
        copies = []
        for d in range(1, n):
            peer = lax.rem(me + d, n)
            copy = pltpu.make_async_remote_copy(
                src_ref=rs.at[k, :, peer],
                dst_ref=got1.at[k, d - 1],
                send_sem=s1_send.at[k, d - 1],
                recv_sem=s1_recv.at[k, d - 1],
                device_id={"strip": peer},
                device_id_type=MESH,
            )
            copy.start()
            copies.append(copy)
        return copies

    def scatter_images(k, before):
        wait_all(before)

        def add(i, carry):
            total = rs[k, i, me]
            for d in range(n - 1):
                total = total + got1[k, d, i]
            part[k, i] = total
            return carry

        lax.fori_loop(0, m, add, 0)
        copies = []
        for d in range(1, m):
            peer = lax.rem(img + d, m)
            copy = pltpu.make_async_remote_copy(
                src_ref=part.at[k, peer],
                dst_ref=got2.at[k, d - 1],
                send_sem=s2_send.at[k, d - 1],
                recv_sem=s2_recv.at[k, d - 1],
                device_id={"img": peer},
                device_id_type=MESH,
            )
            copy.start()
            copies.append(copy)
        return copies

    def gather_strips(k, before):
        wait_all(before)
        total = part[k, img]
        for d in range(m - 1):
            total = total + got2[k, d]
        ag[k, me] = total
        copies = []
        for d in range(1, n):
            copy = pltpu.make_async_remote_copy(
                src_ref=ag.at[k, me],
                dst_ref=ag.at[k, me],
                send_sem=s3_send.at[k, d - 1],
                recv_sem=s3_recv.at[k, d - 1],
                device_id={"strip": lax.rem(me + d, n)},
                device_id_type=MESH,
            )
            copy.start()
            copies.append(copy)
        return copies

    def finish_grad(k, before, target):
        wait_all(before)
        for s in range(n):
            low = min(s * quota, rows_out)
            high = min(low + quota, rows_out)
            if high > low:
                target[low:high] = ag[k, s, 0 : high - low]

    edge[0] = x_ref[0, last]
    edge[1] = g_ref[0, last]
    block = local_stats(lambda r: x_ref[0, r].astype(F32))
    pl.semaphore_wait(barrier, n - 1 + m - 1)
    stats1 = send_block(0, block)
    halo_x = send_halo(0, x_ref.at[0, 0], edge.at[0])
    halo_g = send_halo(1, g_ref.at[0, 0], edge.at[1])

    load_forward(w1_ref)
    for k in (0, 1, slots + 2, slots + 3, slots + 4, slots + 5):
        gt[k] = jnp.zeros((chans, cols), BF16)

    def turn_cotangent(r, carry):
        gt[r + 2] = jnp.where(live(r), g_ref[0, r].astype(F32), 0.0).T.astype(BF16)
        return carry

    lax.fori_loop(0, slots, turn_cotangent, 0, unroll=2)
    wait_all(halo_g)
    build(bufd, 1, lambda r: g_ref[0, r], lambda v: v)
    wait_all(halo_x)
    wait_all(stats1)

    gain1, shift1 = gain1_ref[...], shift1_ref[...]
    gain2, shift2 = gain2_ref[...], shift2_ref[...]
    mean1, inv1 = joined_stats(0)

    def act_one(v):
        pre = (v - mean1) * inv1 * gain1 + shift1
        return pre * sigmoid(pre)

    build(buf1, 0, lambda r: x_ref[0, r], act_one)
    convolve(buf1, hidden)
    stats2 = send_block(1, local_stats(lambda r: hidden[r]))
    load_backward(w2_ref)
    convolve(bufd, back)
    wait_all(stats2)
    mean2, inv2 = joined_stats(1)

    def slope_two(r, carry):
        sum_plain, sum_cross = carry
        normed = (hidden[r] - mean2) * inv2
        pre = normed * gain2 + shift2
        logistic = sigmoid(pre)
        act2[r] = (pre * logistic).astype(BF16)
        slope = logistic * (1.0 + pre * (1.0 - logistic))
        dpre = jnp.where(live(r), back[r] * slope, 0.0)
        back[r] = dpre
        return sum_plain + fold(dpre), sum_cross + fold(dpre * normed)

    sum_plain, sum_cross = lax.fori_loop(0, slots, slope_two, (zero8, zero8))
    edge[2] = act2[last]
    halo_a = send_halo(2, act2.at[0], edge.at[2])
    sums2 = send_block(2, by_row([flat(sum_plain), flat(sum_cross)]))
    load_backward(w1_ref)
    wait_all(halo_a)
    build(buf2, 2, lambda r: act2[r], lambda v: v)
    kernel_grad(buf2)
    stage = scatter_strips(1)
    wait_all(sums2)
    total2 = joined_sums(2)
    mean_plain2, mean_cross2 = means_of(total2, gain2)

    def hidden_grad(r, carry):
        normed = (hidden[r] - mean2) * inv2
        value = inv2 * (back[r] * gain2 - mean_plain2 - normed * mean_cross2)
        value = jnp.where(live(r), value, 0.0)
        dh[r] = value.astype(BF16)
        gt[r + 2] = value.T.astype(BF16)
        return carry

    lax.fori_loop(0, slots, hidden_grad, 0)
    edge[3] = dh[last]
    halo_d = send_halo(3, dh.at[0], edge.at[3])
    kernel_grad(buf1)
    stage_one = scatter_strips(0)
    stage = scatter_images(1, stage)
    wait_all(halo_d)
    build(bufd, 3, lambda r: dh[r], lambda v: v)
    convolve(bufd, back)
    stage = gather_strips(1, stage)

    def slope_one(r, carry):
        sum_plain, sum_cross = carry
        normed = (x_ref[0, r].astype(F32) - mean1) * inv1
        pre = normed * gain1 + shift1
        logistic = sigmoid(pre)
        slope = logistic * (1.0 + pre * (1.0 - logistic))
        dpre = jnp.where(live(r), back[r] * slope, 0.0)
        back[r] = dpre
        return sum_plain + fold(dpre), sum_cross + fold(dpre * normed)

    sum_plain, sum_cross = lax.fori_loop(0, slots, slope_one, (zero8, zero8))
    sums1 = send_block(3, by_row([flat(sum_plain), flat(sum_cross)]))
    stage_one = scatter_images(0, stage_one)
    wait_all(sums1)
    total1 = joined_sums(3)
    mean_plain1, mean_cross1 = means_of(total1, gain1)

    def spread8(row):
        return jnp.broadcast_to(row, (8, chans))

    nbuf[img] = by_row(
        [spread8(total1[1:2]), spread8(total1[0:1]), spread8(total2[1:2]), spread8(total2[0:1])]
    )
    norms = []
    for d in range(1, m):
        copy = pltpu.make_async_remote_copy(
            src_ref=nbuf.at[img],
            dst_ref=nbuf.at[img],
            send_sem=n_send.at[d - 1],
            recv_sem=n_recv.at[d - 1],
            device_id={"img": lax.rem(img + d, m)},
            device_id_type=MESH,
        )
        copy.start()
        norms.append(copy)

    def image_grad(r, carry):
        normed = (x_ref[0, r].astype(F32) - mean1) * inv1
        branch = inv1 * (back[r] * gain1 - mean_plain1 - normed * mean_cross1)
        value = g_ref[0, r].astype(F32) + branch
        out_ref[0, r] = jnp.where(live(r), value, 0.0).astype(BF16)
        return carry

    lax.fori_loop(0, slots, image_grad, 0, unroll=2)
    stage_one = gather_strips(0, stage_one)
    finish_grad(1, stage, grad2_ref)
    wait_all(norms)
    total = nbuf[0]
    for i in range(1, m):
        total = total + nbuf[i]
    norm_ref[...] = total[0:4]
    finish_grad(0, stage_one, grad1_ref)


def body(
    image_in,
    cotangent,
    conv1_w,
    conv2_w,
    norm1_gain,
    norm1_shift,
    norm2_gain,
    norm2_shift,
    strip_rows,
):
    n = lax.axis_size("strip")
    m = lax.axis_size("img")
    _, slots, cols, chans = image_in.shape
    rows_out = 9 * chans // m
    quota = ceil_to(-(-rows_out // n), 8)
    vmem = pl.BlockSpec(memory_space=pltpu.VMEM)
    padded = slots + 4
    scratch = [
        pltpu.VMEM((padded, cols, 3 * chans), BF16),
        pltpu.VMEM((padded, cols, 3 * chans), BF16),
        pltpu.VMEM((padded, cols, 3 * chans), BF16),
        pltpu.VMEM((slots, cols, chans), F32),
        pltpu.VMEM((slots, cols, chans), F32),
        pltpu.VMEM((slots, cols, chans), BF16),
        pltpu.VMEM((slots, cols, chans), BF16),
        pltpu.VMEM((slots + 6, chans, cols), BF16),
        pltpu.VMEM((12 * chans, 2 * chans), BF16),
        pltpu.VMEM((3 * chans, 3 * chans), F32),
        pltpu.VMEM((9 * chans, chans), F32),
        pltpu.VMEM((4, cols, chans), BF16),
        pltpu.VMEM((4, 2, cols, chans), BF16),
        pltpu.VMEM((4, n, 8, chans), F32),
        pltpu.VMEM((m, 8, chans), F32),
        pltpu.VMEM((2, m, n, quota, chans), F32),
        pltpu.VMEM((2, n - 1, m, quota, chans), F32),
        pltpu.VMEM((2, m, quota, chans), F32),
        pltpu.VMEM((2, m - 1, quota, chans), F32),
        pltpu.VMEM((2, n, quota, chans), F32),
        pltpu.SemaphoreType.DMA((4, 2)),
        pltpu.SemaphoreType.DMA((4, 2)),
        pltpu.SemaphoreType.DMA((4, n - 1)),
        pltpu.SemaphoreType.DMA((4, n - 1)),
        pltpu.SemaphoreType.DMA((m - 1,)),
        pltpu.SemaphoreType.DMA((m - 1,)),
        pltpu.SemaphoreType.DMA((2, n - 1)),
        pltpu.SemaphoreType.DMA((2, n - 1)),
        pltpu.SemaphoreType.DMA((2, m - 1)),
        pltpu.SemaphoreType.DMA((2, m - 1)),
        pltpu.SemaphoreType.DMA((2, n - 1)),
        pltpu.SemaphoreType.DMA((2, n - 1)),
    ]
    return pl.pallas_call(
        functools.partial(kernel, n, m, rows_out, quota),
        out_shape=(
            jax.ShapeDtypeStruct(image_in.shape, BF16),
            jax.ShapeDtypeStruct((rows_out, chans), F32),
            jax.ShapeDtypeStruct((rows_out, chans), F32),
            jax.ShapeDtypeStruct((4, chans), F32),
        ),
        in_specs=[pl.BlockSpec(memory_space=pltpu.SMEM)] + [vmem] * 8,
        out_specs=(vmem,) * 4,
        scratch_shapes=scratch,
        compiler_params=pltpu.CompilerParams(
            collective_id=0, has_side_effects=True, vmem_limit_bytes=56 * 1024 * 1024
        ),
    )(
        strip_rows,
        image_in,
        cotangent,
        conv1_w,
        conv2_w,
        norm1_gain.reshape(1, chans),
        norm1_shift.reshape(1, chans),
        norm2_gain.reshape(1, chans),
        norm2_shift.reshape(1, chans),
    )


def solution(mesh):
    placed = (
        P("img", "strip", None, None),
        P("img", "strip", None, None),
        P(),
        P(),
        P(),
        P(),
        P(),
        P(),
        P("img", "strip"),
    )
    return jax.shard_map(
        body,
        mesh=mesh,
        in_specs=placed,
        out_specs=(P("img", "strip", None, None), P("img", None), P("img", None), P()),
        check_vma=False,
    )
```

profile of v0, /device:TPU:0, one launch (start us, length us, event | category | flops | bytes accessed | tf_op | source)
XLA Modules:
  0.0 77.7 jit_solution(1018601850552227464)
XLA Ops:
  1.3 71.9 %shard_map.120 = (bf16[1,32,128,128]{3,2,1,0:T(8,128)(2,1)}, f32[144,128]{1,0:T(8,128)}, f32[144,128]{1,0:T(8,128)}, f32[4,128]{1,0:T(4,128)}) custom-call(s32[1,1]{1,0:T(1,128)S(6)} %copy.17.len_ref, bf16[1,32,128,128]{3,2,1,0:T(8,128)(2,1)} %x_ref.1, bf16[1,32,128,128]{3,2,1,0:T(8,128)(2,1)} %g_ref.1, bf16[3,3,128,128]{3,2,1,0:T(8,128)(2,1)} %w1_ref.1, ...), custom_call_target="tpu_custom_call" | custom-call | tf_op jit(solution)/shard_map/pallas_call | solution.py:569
  73.2 0.0 copy-start.1
  73.2 2.3 %copy.18 = bf16[1,32,128,128]{3,2,1,0:T(8,128)(2,1)} copy(bf16[1,32,128,128]{3,2,1,0:T(8,128)(2,1)} %get-tuple-element.8) | data formatting | bytes 2097152
  75.6 0.0 copy-done.1
  75.6 0.0 copy-start
  75.6 0.6 copy.19
  76.2 0.3 copy-done
  76.5 0.0 copy-start.2
  76.5 0.6 copy.20
  77.1 0.0 copy-done.2
  77.2 0.6 copy.21
Async XLA Ops:
  73.2 2.4 %copy-start.1 = (f32[144,128]{1,0:T(8,128)S(1)}, f32[144,128]{1,0:T(8,128)}, u32[]{:S(2)}) copy-start(f32[144,128]{1,0:T(8,128)} %get-tuple-element.9) | copy-start | bytes 221188
  75.6 0.9 %copy-start = (f32[144,128]{1,0:T(8,128)S(1)}, f32[144,128]{1,0:T(8,128)}, u32[]{:S(2)}) copy-start(f32[144,128]{1,0:T(8,128)} %get-tuple-element.10) | copy-start | bytes 221188
  76.5 0.7 copy-start.2
where the time goes:
time: 78 us; the launch traced here: 77.7 us
  Pallas kernels  71.9 us (92%)
  local copies, waits for them, and re-layouts  4.51 us (6%)
  between operations  1.3 us (2%)
    pallas_call x1, Pallas kernels, body(): pl.pallas_call(functools.partial(kernel, n, m, rows_out, quota), out_shap...  71.9 us
    unnamed x10, local copies, waits for them, and re-layouts  4.51 us

commit v1 on v0

--- a/solution.py
+++ b/solution.py
@@ -12,10 +12,6 @@
 F32 = jnp.float32
 BF16 = jnp.bfloat16
 MESH = pl.DeviceIdType.MESH
-
-
-def ceil_to(value, unit):
-    return -(-value // unit) * unit
 
 
 def sigmoid(z):
@@ -54,7 +50,6 @@
     n,
     m,
     rows_out,
-    quota,
     len_ref,
     x_ref,
     g_ref,
@@ -84,10 +79,9 @@
     xbuf,
     nbuf,
     rs,
-    got1,
-    part,
-    got2,
+    got,
     ag,
+    corr,
     halo_send,
     halo_recv,
     x_send,
@@ -98,8 +92,6 @@
     s1_recv,
     s2_send,
     s2_recv,
-    s3_send,
-    s3_recv,
 ):
     _, slots, cols, chans = x_ref.shape
     size = chans // GROUPS
@@ -137,9 +129,21 @@
             device_id={"strip": lax.rem(me + n - 1, n)},
             device_id_type=MESH,
         )
-        below.start()
-        above.start()
-        return [below, above]
+        pl.when(me < n - 1)(below.start)
+        pl.when(me > 0)(above.start)
+
+        def wait():
+            @pl.when(me < n - 1)
+            def _():
+                below.wait_send()
+                above.wait_recv()
+
+            @pl.when(me > 0)
+            def _():
+                above.wait_send()
+                below.wait_recv()
+
+        return wait
 
     def send_block(kind, block):
         xbuf[kind, me] = block
@@ -211,7 +215,28 @@
     has_above = jnp.where(me > 0, 1, 0)
     has_below = jnp.where(me < n - 1, 1, 0)
 
-    def build(buf, kind, load, change):
+    def shifted(value):
+        before = jnp.where(column == 0, 0.0, pltpu.roll(value, 1, 0))
+        after = jnp.where(column == cols - 1, 0.0, pltpu.roll(value, cols - 1, 0))
+        return before.astype(BF16), value.astype(BF16), after.astype(BF16)
+
+    def put(buf, i, value):
+        for b, piece in enumerate(shifted(value)):
+            buf[i, :, b * chans : (b + 1) * chans] = piece
+
+    def clear(buf, i):
+        buf[i] = jnp.zeros((cols, 3 * chans), BF16)
+
+    def build(buf, load):
+        def one_row(r, carry):
+            put(buf, r + 1, load(r))
+            return carry
+
+        lax.fori_loop(0, slots, one_row, 0, unroll=2)
+        clear(buf, 0)
+        clear(buf, slots + 1)
+
+    def build_joined(buf, kind, load, change):
         def one_row(i, carry):
             r = i - 1
             own = load(jnp.clip(r, 0, slots - 1)).astype(F32)
@@ -220,28 +245,48 @@
             value = jnp.where(at == length, halo[kind, 1].astype(F32), value)
             keep = jnp.where(at < 0, has_above, jnp.where(at == length, has_below, 1))
             keep = jnp.where(at > length, 0, keep)
-            value = jnp.where(keep > 0, change(value), 0.0)
-            before = jnp.where(column == 0, 0.0, pltpu.roll(value, 1, 0))
-            after = jnp.where(column == cols - 1, 0.0, pltpu.roll(value, cols - 1, 0))
-            buf[i, :, 0:chans] = before.astype(BF16)
-            buf[i, :, chans : 2 * chans] = value.astype(BF16)
-            buf[i, :, 2 * chans : 3 * chans] = after.astype(BF16)
+            put(buf, i, jnp.where(keep > 0, change(value), 0.0))
             return carry
 
         lax.fori_loop(0, slots + 2, one_row, 0, unroll=2)
-        buf[slots + 2] = jnp.zeros((cols, 3 * chans), BF16)
-        buf[slots + 3] = jnp.zeros((cols, 3 * chans), BF16)
-
-    def load_forward(w_ref):
+
+    def arrived(kind):
+        flags = (has_above, has_below)
+        return [
+            jnp.concatenate(
+                shifted(
+                    jnp.where(
+                        jnp.full((cols, chans), flags[e], jnp.int32) > 0,
+                        halo[kind, e].astype(F32),
+                        0.0,
+                    )
+                ),
+                axis=1,
+            )
+            for e in range(2)
+        ]
+
+    def edge_terms(kind, w):
+        top, bottom = arrived(kind)
+        taps = 3 * chans
+        corr[0] = jnp.dot(top, wp[w, 0:taps, 0:chans], preferred_element_type=F32)
+        corr[1] = jnp.dot(bottom, wp[w, 2 * taps : 3 * taps, 0:chans], preferred_element_type=F32)
+
+    def with_edges(r):
+        at = jnp.full((cols, chans), r, jnp.int32)
+        value = back[r] + jnp.where(at == 0, corr[0], 0.0)
+        return value + jnp.where(at == last, corr[1], 0.0)
+
+    def load_forward(w, w_ref):
         for j in range(4):
             for b in range(3):
                 at = (j * 3 + b) * chans
                 for t in range(2):
                     a = j - t
                     tap = w_ref[a, b] if 0 <= a <= 2 else jnp.zeros((chans, chans), BF16)
-                    wp[at : at + chans, t * chans : (t + 1) * chans] = tap
-
-    def load_backward(w_ref):
+                    wp[w, at : at + chans, t * chans : (t + 1) * chans] = tap
+
+    def load_backward(w, w_ref):
         for j in range(4):
             for b in range(3):
                 at = (j * 3 + b) * chans
@@ -251,11 +296,11 @@
                         tap = w_ref[2 - a, 2 - b].astype(F32).T.astype(BF16)
                     else:
                         tap = jnp.zeros((chans, chans), BF16)
-                    wp[at : at + chans, t * chans : (t + 1) * chans] = tap
-
-    pairs = 4
-
-    def convolve(buf, out):
+                    wp[w, at : at + chans, t * chans : (t + 1) * chans] = tap
+
+    pairs = slots // 4
+
+    def convolve(buf, w, out):
         def step(q, carry):
             base = q * (2 * pairs)
             pieces = []
@@ -264,7 +309,7 @@
                     jnp.concatenate([buf[base + (2 * p + j)] for j in range(4)], axis=1)
                 )
             result = jnp.dot(
-                jnp.concatenate(pieces, axis=0), wp[...], preferred_element_type=F32
+                jnp.concatenate(pieces, axis=0), wp[w], preferred_element_type=F32
             )
             for p in range(pairs):
                 for t in range(2):
@@ -277,21 +322,26 @@
 
     def kernel_grad(buf):
         acc[...] = jnp.zeros_like(acc)
-        rows = 4
+        rows = 8
 
         def step(q, carry):
+            base = q * rows + 1
             left = jnp.concatenate(
                 [
-                    jnp.concatenate([gt[q * rows + (k + 2 - a)] for k in range(rows)], axis=1)
+                    jnp.concatenate([gt[base + (k + 2 - a)] for k in range(rows)], axis=1)
                     for a in range(3)
                 ],
                 axis=0,
             )
-            right = jnp.concatenate([buf[q * rows + k] for k in range(rows)], axis=0)
+            right = jnp.concatenate([buf[base + k] for k in range(rows)], axis=0)
             acc[...] += jnp.dot(left, right, preferred_element_type=F32)
             return carry
 
-        lax.fori_loop(0, (slots + 4) // rows, step, 0)
+        lax.fori_loop(0, slots // rows, step, 0)
+
+    def edge_grads(top, bottom, turned):
+        acc[0:chans] += jnp.dot(gt[2], top, preferred_element_type=F32)
+        acc[2 * chans :] += jnp.dot(turned, bottom, preferred_element_type=F32)
         for a in range(3):
             for b in range(3):
                 at = (a * 3 + b) * chans
@@ -299,51 +349,17 @@
                     a * chans : (a + 1) * chans, b * chans : (b + 1) * chans
                 ].T
 
-    def scatter_strips(k):
+    def scatter_images(k):
         for i in range(m):
-            for s in range(n):
-                low = min(s * quota, rows_out)
-                high = min(low + quota, rows_out)
-                if high > low:
-                    rs[k, i, s, 0 : high - low] = full[i * rows_out + low : i * rows_out + high]
-                if high - low < quota:
-                    rs[k, i, s, high - low : quota] = jnp.zeros(
-                        (quota - (high - low), chans), F32
-                    )
-        copies = []
-        for d in range(1, n):
-            peer = lax.rem(me + d, n)
-            copy = pltpu.make_async_remote_copy(
-                src_ref=rs.at[k, :, peer],
-                dst_ref=got1.at[k, d - 1],
-                send_sem=s1_send.at[k, d - 1],
-                recv_sem=s1_recv.at[k, d - 1],
-                device_id={"strip": peer},
-                device_id_type=MESH,
-            )
-            copy.start()
-            copies.append(copy)
-        return copies
-
-    def scatter_images(k, before):
-        wait_all(before)
-
-        def add(i, carry):
-            total = rs[k, i, me]
-            for d in range(n - 1):
-                total = total + got1[k, d, i]
-            part[k, i] = total
-            return carry
-
-        lax.fori_loop(0, m, add, 0)
+            rs[k, i] = full[i * rows_out : (i + 1) * rows_out].astype(BF16)
         copies = []
         for d in range(1, m):
             peer = lax.rem(img + d, m)
             copy = pltpu.make_async_remote_copy(
-                src_ref=part.at[k, peer],
-                dst_ref=got2.at[k, d - 1],
-                send_sem=s2_send.at[k, d - 1],
-                recv_sem=s2_recv.at[k, d - 1],
+                src_ref=rs.at[k, peer],
+                dst_ref=got.at[k, d - 1],
+                send_sem=s1_send.at[k, d - 1],
+                recv_sem=s1_recv.at[k, d - 1],
                 device_id={"img": peer},
                 device_id_type=MESH,
             )
@@ -351,19 +367,19 @@
             copies.append(copy)
         return copies
 
-    def gather_strips(k, before):
+    def share_strips(k, before):
         wait_all(before)
-        total = part[k, img]
+        total = rs[k, img].astype(F32)
         for d in range(m - 1):
-            total = total + got2[k, d]
-        ag[k, me] = total
+            total = total + got[k, d].astype(F32)
+        ag[k, me] = total.astype(BF16)
         copies = []
         for d in range(1, n):
             copy = pltpu.make_async_remote_copy(
                 src_ref=ag.at[k, me],
                 dst_ref=ag.at[k, me],
-                send_sem=s3_send.at[k, d - 1],
-                recv_sem=s3_recv.at[k, d - 1],
+                send_sem=s2_send.at[k, d - 1],
+                recv_sem=s2_recv.at[k, d - 1],
                 device_id={"strip": lax.rem(me + d, n)},
                 device_id_type=MESH,
             )
@@ -373,47 +389,49 @@
 
     def finish_grad(k, before, target):
         wait_all(before)
-        for s in range(n):
-            low = min(s * quota, rows_out)
-            high = min(low + quota, rows_out)
-            if high > low:
-                target[low:high] = ag[k, s, 0 : high - low]
+        total = ag[k, 0].astype(F32)
+        for s in range(1, n):
+            total = total + ag[k, s].astype(F32)
+        target[...] = total
 
     edge[0] = x_ref[0, last]
     edge[1] = g_ref[0, last]
     block = local_stats(lambda r: x_ref[0, r].astype(F32))
+    build(bufd, lambda r: jnp.where(live(r), g_ref[0, r].astype(F32), 0.0))
+    load_backward(1, w2_ref)
     pl.semaphore_wait(barrier, n - 1 + m - 1)
     stats1 = send_block(0, block)
     halo_x = send_halo(0, x_ref.at[0, 0], edge.at[0])
     halo_g = send_halo(1, g_ref.at[0, 0], edge.at[1])
 
-    load_forward(w1_ref)
-    for k in (0, 1, slots + 2, slots + 3, slots + 4, slots + 5):
+    convolve(bufd, 1, back)
+    load_forward(0, w1_ref)
+    halo_x()
+    wait_all(stats1)
+
+    gain1, shift1 = gain1_ref[...], shift1_ref[...]
+    gain2, shift2 = gain2_ref[...], shift2_ref[...]
+    mean1, inv1 = joined_stats(0)
+
+    def act_one(v):
+        pre = (v - mean1) * inv1 * gain1 + shift1
+        return pre * sigmoid(pre)
+
+    build_joined(buf1, 0, lambda r: x_ref[0, r], act_one)
+    convolve(buf1, 0, hidden)
+    stats2 = send_block(1, local_stats(lambda r: hidden[r]))
+
+    for k in (0, 1, slots + 2, slots + 3):
         gt[k] = jnp.zeros((chans, cols), BF16)
 
     def turn_cotangent(r, carry):
         gt[r + 2] = jnp.where(live(r), g_ref[0, r].astype(F32), 0.0).T.astype(BF16)
         return carry
 
-    lax.fori_loop(0, slots, turn_cotangent, 0, unroll=2)
-    wait_all(halo_g)
-    build(bufd, 1, lambda r: g_ref[0, r], lambda v: v)
-    wait_all(halo_x)
-    wait_all(stats1)
-
-    gain1, shift1 = gain1_ref[...], shift1_ref[...]
-    gain2, shift2 = gain2_ref[...], shift2_ref[...]
-    mean1, inv1 = joined_stats(0)
-
-    def act_one(v):
-        pre = (v - mean1) * inv1 * gain1 + shift1
-        return pre * sigmoid(pre)
-
-    build(buf1, 0, lambda r: x_ref[0, r], act_one)
-    convolve(buf1, hidden)
-    stats2 = send_block(1, local_stats(lambda r: hidden[r]))
-    load_backward(w2_ref)
-    convolve(bufd, back)
+    lax.fori_loop(0, slots, turn_cotangent, 0, unroll=4)
+    load_backward(2, w1_ref)
+    halo_g()
+    edge_terms(1, 1)
     wait_all(stats2)
     mean2, inv2 = joined_stats(1)
 
@@ -424,20 +442,21 @@
         logistic = sigmoid(pre)
         act2[r] = (pre * logistic).astype(BF16)
         slope = logistic * (1.0 + pre * (1.0 - logistic))
-        dpre = jnp.where(live(r), back[r] * slope, 0.0)
+        dpre = jnp.where(live(r), with_edges(r) * slope, 0.0)
         back[r] = dpre
         return sum_plain + fold(dpre), sum_cross + fold(dpre * normed)
 
     sum_plain, sum_cross = lax.fori_loop(0, slots, slope_two, (zero8, zero8))
     edge[2] = act2[last]
+    sums2 = send_block(2, by_row([flat(sum_plain), flat(sum_cross)]))
     halo_a = send_halo(2, act2.at[0], edge.at[2])
-    sums2 = send_block(2, by_row([flat(sum_plain), flat(sum_cross)]))
-    load_backward(w1_ref)
-    wait_all(halo_a)
-    build(buf2, 2, lambda r: act2[r], lambda v: v)
+    build(buf2, lambda r: jnp.where(live(r), act2[r].astype(F32), 0.0))
     kernel_grad(buf2)
-    stage = scatter_strips(1)
+    halo_a()
+    top, bottom = arrived(2)
+    edge_grads(top, bottom, gt[last + 2])
     wait_all(sums2)
+    stage_two = scatter_images(1)
     total2 = joined_sums(2)
     mean_plain2, mean_cross2 = means_of(total2, gain2)
 
@@ -449,16 +468,17 @@
         gt[r + 2] = value.T.astype(BF16)
         return carry
 
-    lax.fori_loop(0, slots, hidden_grad, 0)
+    lax.fori_loop(0, slots, hidden_grad, 0, unroll=2)
     edge[3] = dh[last]
     halo_d = send_halo(3, dh.at[0], edge.at[3])
     kernel_grad(buf1)
-    stage_one = scatter_strips(0)
-    stage = scatter_images(1, stage)
-    wait_all(halo_d)
-    build(bufd, 3, lambda r: dh[r], lambda v: v)
-    convolve(bufd, back)
-    stage = gather_strips(1, stage)
+    edge_grads(buf1[0], buf1[slots + 1], gt[slots + 1])
+    stage_one = scatter_images(0)
+    stage_two = share_strips(1, stage_two)
+    build(bufd, lambda r: dh[r].astype(F32))
+    convolve(bufd, 2, back)
+    halo_d()
+    edge_terms(3, 2)
 
     def slope_one(r, carry):
         sum_plain, sum_cross = carry
@@ -466,13 +486,14 @@
         pre = normed * gain1 + shift1
         logistic = sigmoid(pre)
         slope = logistic * (1.0 + pre * (1.0 - logistic))
-        dpre = jnp.where(live(r), back[r] * slope, 0.0)
+        dpre = jnp.where(live(r), with_edges(r) * slope, 0.0)
         back[r] = dpre
         return sum_plain + fold(dpre), sum_cross + fold(dpre * normed)
 
     sum_plain, sum_cross = lax.fori_loop(0, slots, slope_one, (zero8, zero8))
     sums1 = send_block(3, by_row([flat(sum_plain), flat(sum_cross)]))
-    stage_one = scatter_images(0, stage_one)
+    stage_one = share_strips(0, stage_one)
+    finish_grad(1, stage_two, grad2_ref)
     wait_all(sums1)
     total1 = joined_sums(3)
     mean_plain1, mean_cross1 = means_of(total1, gain1)
@@ -504,8 +525,6 @@
         return carry
 
     lax.fori_loop(0, slots, image_grad, 0, unroll=2)
-    stage_one = gather_strips(0, stage_one)
-    finish_grad(1, stage, grad2_ref)
     wait_all(norms)
     total = nbuf[0]
     for i in range(1, m):
@@ -529,9 +548,8 @@
     m = lax.axis_size("img")
     _, slots, cols, chans = image_in.shape
     rows_out = 9 * chans // m
-    quota = ceil_to(-(-rows_out // n), 8)
     vmem = pl.BlockSpec(memory_space=pltpu.VMEM)
-    padded = slots + 4
+    padded = slots + 2
     scratch = [
         pltpu.VMEM((padded, cols, 3 * chans), BF16),
         pltpu.VMEM((padded, cols, 3 * chans), BF16),
@@ -540,34 +558,31 @@
         pltpu.VMEM((slots, cols, chans), F32),
         pltpu.VMEM((slots, cols, chans), BF16),
         pltpu.VMEM((slots, cols, chans), BF16),
-        pltpu.VMEM((slots + 6, chans, cols), BF16),
-        pltpu.VMEM((12 * chans, 2 * chans), BF16),
+        pltpu.VMEM((slots + 4, chans, cols), BF16),
+        pltpu.VMEM((3, 12 * chans, 2 * chans), BF16),
         pltpu.VMEM((3 * chans, 3 * chans), F32),
         pltpu.VMEM((9 * chans, chans), F32),
         pltpu.VMEM((4, cols, chans), BF16),
         pltpu.VMEM((4, 2, cols, chans), BF16),
         pltpu.VMEM((4, n, 8, chans), F32),
         pltpu.VMEM((m, 8, chans), F32),
-        pltpu.VMEM((2, m, n, quota, chans), F32),
-        pltpu.VMEM((2, n - 1, m, quota, chans), F32),
-        pltpu.VMEM((2, m, quota, chans), F32),
-        pltpu.VMEM((2, m - 1, quota, chans), F32),
-        pltpu.VMEM((2, n, quota, chans), F32),
+        pltpu.VMEM((2, m, rows_out, chans), BF16),
+        pltpu.VMEM((2, m - 1, rows_out, chans), BF16),
+        pltpu.VMEM((2, n, rows_out, chans), BF16),
+        pltpu.VMEM((2, cols, chans), F32),
         pltpu.SemaphoreType.DMA((4, 2)),
         pltpu.SemaphoreType.DMA((4, 2)),
         pltpu.SemaphoreType.DMA((4, n - 1)),
         pltpu.SemaphoreType.DMA((4, n - 1)),
         pltpu.SemaphoreType.DMA((m - 1,)),
         pltpu.SemaphoreType.DMA((m - 1,)),
-        pltpu.SemaphoreType.DMA((2, n - 1)),
-        pltpu.SemaphoreType.DMA((2, n - 1)),
         pltpu.SemaphoreType.DMA((2, m - 1)),
         pltpu.SemaphoreType.DMA((2, m - 1)),
         pltpu.SemaphoreType.DMA((2, n - 1)),
         pltpu.SemaphoreType.DMA((2, n - 1)),
     ]
     return pl.pallas_call(
-        functools.partial(kernel, n, m, rows_out, quota),
+        functools.partial(kernel, n, m, rows_out),
         out_shape=(
             jax.ShapeDtypeStruct(image_in.shape, BF16),
             jax.ShapeDtypeStruct((rows_out, chans), F32),
@@ -578,7 +593,7 @@
         out_specs=(vmem,) * 4,
         scratch_shapes=scratch,
         compiler_params=pltpu.CompilerParams(
-            collective_id=0, has_side_effects=True, vmem_limit_bytes=56 * 1024 * 1024
+            collective_id=0, has_side_effects=True, vmem_limit_bytes=32 * 1024 * 1024
         ),
     )(
         strip_rows,

time: 78 us -> 49.7 us (0.64)
  Pallas kernels: 71.9 us -> 40.3 us
  local copies, waits for them, and re-layouts: 4.51 us -> 7.86 us
    pallas_call x1, Pallas kernels: 71.9 us -> 40.3 us  [body(): pl.pallas_call(functools.partial(kernel, n, m, rows_out), out_shape=(jax....]
    unnamed x10 -> x20, local copies, waits for them, and re-layouts: 4.51 us -> 7.86 us
where the time goes in v1:
time: 49.7 us; the launch traced here: 49.5 us
  Pallas kernels  40.3 us (81%)
  local copies, waits for them, and re-layouts  7.86 us (16%)
  between operations  1.33 us (3%)
    pallas_call x1, Pallas kernels, body(): pl.pallas_call(functools.partial(kernel, n, m, rows_out), out_shape=(jax....  40.3 us
    unnamed x20, local copies, waits for them, and re-layouts  7.86 us

profile of v1, /device:TPU:0, one launch (start us, length us, event | category | flops | bytes accessed | tf_op | source)
XLA Modules:
  0.0 49.5 jit_solution(1356432719449292341)
XLA Ops:
  1.3 0.0 copy-start.7
  1.3 0.0 copy-start.4
  1.3 0.0 copy-start.5
  1.3 0.0 copy-start.6
  1.3 0.6 %copy-done.7 = f32[128]{0:T(128)S(1)} copy-done((f32[128]{0:T(128)S(1)}, f32[128]{0:T(128)}, u32[]{:S(2)}) %copy-start.7) | copy-done | bytes 536
  1.9 0.0 copy-done.4
  2.0 0.0 copy-done.5
  2.0 0.0 copy-done.6
  2.0 0.0 copy-start
  2.0 1.2 %copy-done = bf16[1,32,128,128]{3,2,1,0:T(8,128)(2,1)S(1)} copy-done((bf16[1,32,128,128]{3,2,1,0:T(8,128)(2,1)S(1)}, bf16[1,32,128,128]{3,2,1,0:T(8,128)(2,1)}, u32[]{:S(2)}) %copy-start) | copy-done | bytes 1048600
  3.2 0.0 copy-start.1
  3.2 1.2 %copy-done.1 = bf16[1,32,128,128]{3,2,1,0:T(8,128)(2,1)S(1)} copy-done((bf16[1,32,128,128]{3,2,1,0:T(8,128)(2,1)S(1)}, bf16[1,32,128,128]{3,2,1,0:T(8,128)(2,1)}, u32[]{:S(2)}) %copy-start.1) | copy-done | bytes 1048600
  4.4 0.0 copy-start.2
  4.4 1.0 %copy-done.2 = bf16[3,3,128,128]{3,2,1,0:T(8,128)(2,1)S(1)} copy-done((bf16[3,3,128,128]{3,2,1,0:T(8,128)(2,1)S(1)}, bf16[3,3,128,128]{3,2,1,0:T(8,128)(2,1)}, u32[]{:S(2)}) %copy-start.2) | copy-done | bytes 294936
  5.4 0.0 copy-start.3
  5.4 1.0 %copy-done.3 = bf16[3,3,128,128]{3,2,1,0:T(8,128)(2,1)S(1)} copy-done((bf16[3,3,128,128]{3,2,1,0:T(8,128)(2,1)S(1)}, bf16[3,3,128,128]{3,2,1,0:T(8,128)(2,1)}, u32[]{:S(2)}) %copy-start.3) | copy-done | bytes 294936
  6.4 40.3 %shard_map.120 = (bf16[1,32,128,128]{3,2,1,0:T(8,128)(2,1)S(1)}, f32[144,128]{1,0:T(8,128)S(1)}, f32[144,128]{1,0:T(8,128)S(1)}, f32[4,128]{1,0:T(4,128)S(1)}) custom-call(s32[1,1]{1,0:T(1,128)S(6)} %copy.17.len_ref, bf16[1,32,128,128]{3,2,1,0:T(8,128)(2,1)S(1)} %copy-done, bf16[1,32,128,128]{3,2,1,0:T(8,128)(2,1)S(1)} %copy-done.1, ...), custom_call_target="tpu_custom_call" | custom-call | tf_op jit(solution)/shard_map/pallas_call | solution.py:584
  46.6 1.0 %copy.18 = bf16[1,32,128,128]{3,2,1,0:T(8,128)(2,1)} copy(bf16[1,32,128,128]{3,2,1,0:T(8,128)(2,1)S(1)} %get-tuple-element.8) | data formatting | bytes 2097152
  47.6 0.6 %copy.19 = f32[144,128]{1,0:T(8,128)} copy(f32[144,128]{1,0:T(8,128)S(1)} %get-tuple-element.9) | data formatting | bytes 147456
  48.2 0.6 %copy.20 = f32[144,128]{1,0:T(8,128)} copy(f32[144,128]{1,0:T(8,128)S(1)} %get-tuple-element.10) | data formatting | bytes 147456
  48.9 0.6 %copy.21 = f32[4,128]{1,0:T(4,128)} copy(f32[4,128]{1,0:T(4,128)S(1)} %get-tuple-element.11) | data formatting | bytes 4096
Async XLA Ops:
  1.3 0.7 %copy-start.7 = (f32[128]{0:T(128)S(1)}, f32[128]{0:T(128)}, u32[]{:S(2)}) copy-start(f32[128]{0:T(128)} %param.16) | copy-start | bytes 1540
  1.3 0.7 %copy-start.4 = (f32[128]{0:T(128)S(1)}, f32[128]{0:T(128)}, u32[]{:S(2)}) copy-start(f32[128]{0:T(128)} %param.13) | copy-start | bytes 1540
  1.3 0.7 %copy-start.5 = (f32[128]{0:T(128)S(1)}, f32[128]{0:T(128)}, u32[]{:S(2)}) copy-start(f32[128]{0:T(128)} %param.14) | copy-start | bytes 1540
  1.3 0.7 %copy-start.6 = (f32[128]{0:T(128)S(1)}, f32[128]{0:T(128)}, u32[]{:S(2)}) copy-start(f32[128]{0:T(128)} %param.15) | copy-start | bytes 1540
  2.0 1.2 %copy-start = (bf16[1,32,128,128]{3,2,1,0:T(8,128)(2,1)S(1)}, bf16[1,32,128,128]{3,2,1,0:T(8,128)(2,1)}, u32[]{:S(2)}) copy-start(bf16[1,32,128,128]{3,2,1,0:T(8,128)(2,1)} %x_ref.1) | copy-start | bytes 3145732
  3.2 1.2 %copy-start.1 = (bf16[1,32,128,128]{3,2,1,0:T(8,128)(2,1)S(1)}, bf16[1,32,128,128]{3,2,1,0:T(8,128)(2,1)}, u32[]{:S(2)}) copy-start(bf16[1,32,128,128]{3,2,1,0:T(8,128)(2,1)} %g_ref.1) | copy-start | bytes 3145732
  4.4 1.0 %copy-start.2 = (bf16[3,3,128,128]{3,2,1,0:T(8,128)(2,1)S(1)}, bf16[3,3,128,128]{3,2,1,0:T(8,128)(2,1)}, u32[]{:S(2)}) copy-start(bf16[3,3,128,128]{3,2,1,0:T(8,128)(2,1)} %w1_ref.1) | copy-start | bytes 884740
  5.4 1.0 %copy-start.3 = (bf16[3,3,128,128]{3,2,1,0:T(8,128)(2,1)S(1)}, bf16[3,3,128,128]{3,2,1,0:T(8,128)(2,1)}, u32[]{:S(2)}) copy-start(bf16[3,3,128,128]{3,2,1,0:T(8,128)(2,1)} %w2_ref.1) | copy-start | bytes 884740

commit v2 on v1

--- a/solution.py
+++ b/solution.py
@@ -11,6 +11,7 @@
 EPSILON = 1e-06
 F32 = jnp.float32
 BF16 = jnp.bfloat16
+CHUNKS = 4
 MESH = pl.DeviceIdType.MESH
 
 
@@ -51,18 +52,24 @@
     m,
     rows_out,
     len_ref,
+    x_hbm,
+    g_hbm,
+    w1_hbm,
+    w2_hbm,
+    gain1_hbm,
+    shift1_hbm,
+    gain2_hbm,
+    shift2_hbm,
+    out_ref,
+    grad1_ref,
+    grad2_ref,
+    norm_ref,
     x_ref,
     g_ref,
     w1_ref,
     w2_ref,
-    gain1_ref,
-    shift1_ref,
-    gain2_ref,
-    shift2_ref,
-    out_ref,
-    grad1_ref,
-    grad2_ref,
-    norm_ref,
+    params,
+    load_sem,
     buf1,
     buf2,
     bufd,
@@ -112,6 +119,22 @@
             barrier, inc=1, device_id={"img": lax.rem(img + d, m)}, device_id_type=MESH
         )
 
+    piece = slots // CHUNKS
+    loads = [
+        pltpu.make_async_copy(
+            x_hbm.at[0, pl.ds(c * piece, piece)],
+            x_ref.at[0, pl.ds(c * piece, piece)],
+            load_sem.at[c],
+        )
+        for c in range(CHUNKS)
+    ]
+    for k, (source, target) in enumerate(((g_hbm, g_ref), (w2_hbm, w2_ref), (w1_hbm, w1_ref))):
+        loads.append(pltpu.make_async_copy(source, target, load_sem.at[CHUNKS + k]))
+    for k, source in enumerate((gain1_hbm, shift1_hbm, gain2_hbm, shift2_hbm)):
+        loads.append(pltpu.make_async_copy(source, params.at[k], load_sem.at[CHUNKS + 3 + k]))
+    for load in loads:
+        load.start()
+
     def send_halo(kind, first, last):
         below = pltpu.make_async_remote_copy(
             src_ref=last,
@@ -170,11 +193,13 @@
 
     zero8 = jnp.zeros((8, chans), F32)
 
-    def local_stats(load):
+    def add_rows(load, start, count, total):
         def add(r, total):
             return total + fold(jnp.where(live(r), load(r), 0.0))
 
-        total = lax.fori_loop(0, slots, add, zero8, unroll=2)
+        return lax.fori_loop(start, start + count, add, total, unroll=2)
+
+    def local_stats(load, total):
         count = (jnp.full((8, chans), length, jnp.int32) * (cols * size)).astype(F32)
         mean = group_sum(flat(total), size) / count
         one = mean[0:1]
@@ -300,7 +325,7 @@
 
     pairs = slots // 4
 
-    def convolve(buf, w, out):
+    def convolve(buf, w, out, summed=False):
         def step(q, carry):
             base = q * (2 * pairs)
             pieces = []
@@ -313,12 +338,14 @@
             )
             for p in range(pairs):
                 for t in range(2):
-                    out[base + (2 * p + t)] = result[
-                        p * cols : (p + 1) * cols, t * chans : (t + 1) * chans
-                    ]
+                    row = base + (2 * p + t)
+                    value = result[p * cols : (p + 1) * cols, t * chans : (t + 1) * chans]
+                    out[row] = value
+                    if summed:
+                        carry = carry + fold(jnp.where(live(row), value, 0.0))
             return carry
 
-        lax.fori_loop(0, slots // (2 * pairs), step, 0)
+        return lax.fori_loop(0, slots // (2 * pairs), step, zero8)
 
     def kernel_grad(buf):
         acc[...] = jnp.zeros_like(acc)
@@ -394,10 +421,19 @@
             total = total + ag[k, s].astype(F32)
         target[...] = total
 
+    def source(r):
+        return x_ref[0, r].astype(F32)
+
+    total = zero8
+    for c in range(CHUNKS):
+        loads[c].wait()
+        total = add_rows(source, c * piece, piece, total)
     edge[0] = x_ref[0, last]
+    block = local_stats(source, total)
+    loads[CHUNKS].wait()
     edge[1] = g_ref[0, last]
-    block = local_stats(lambda r: x_ref[0, r].astype(F32))
     build(bufd, lambda r: jnp.where(live(r), g_ref[0, r].astype(F32), 0.0))
+    loads[CHUNKS + 1].wait()
     load_backward(1, w2_ref)
     pl.semaphore_wait(barrier, n - 1 + m - 1)
     stats1 = send_block(0, block)
@@ -405,12 +441,14 @@
     halo_g = send_halo(1, g_ref.at[0, 0], edge.at[1])
 
     convolve(bufd, 1, back)
+    loads[CHUNKS + 2].wait()
     load_forward(0, w1_ref)
     halo_x()
     wait_all(stats1)
 
-    gain1, shift1 = gain1_ref[...], shift1_ref[...]
-    gain2, shift2 = gain2_ref[...], shift2_ref[...]
+    for k in range(4):
+        loads[CHUNKS + 3 + k].wait()
+    gain1, shift1, gain2, shift2 = params[0], params[1], params[2], params[3]
     mean1, inv1 = joined_stats(0)
 
     def act_one(v):
@@ -418,8 +456,8 @@
         return pre * sigmoid(pre)
 
     build_joined(buf1, 0, lambda r: x_ref[0, r], act_one)
-    convolve(buf1, 0, hidden)
-    stats2 = send_block(1, local_stats(lambda r: hidden[r]))
+    total = convolve(buf1, 0, hidden, summed=True)
+    stats2 = send_block(1, local_stats(lambda r: hidden[r], total))
 
     for k in (0, 1, slots + 2, slots + 3):
         gt[k] = jnp.zeros((chans, cols), BF16)
@@ -446,7 +484,7 @@
         back[r] = dpre
         return sum_plain + fold(dpre), sum_cross + fold(dpre * normed)
 
-    sum_plain, sum_cross = lax.fori_loop(0, slots, slope_two, (zero8, zero8))
+    sum_plain, sum_cross = lax.fori_loop(0, slots, slope_two, (zero8, zero8), unroll=2)
     edge[2] = act2[last]
     sums2 = send_block(2, by_row([flat(sum_plain), flat(sum_cross)]))
     halo_a = send_halo(2, act2.at[0], edge.at[2])
@@ -474,8 +512,8 @@
     kernel_grad(buf1)
     edge_grads(buf1[0], buf1[slots + 1], gt[slots + 1])
     stage_one = scatter_images(0)
+    build(bufd, lambda r: dh[r].astype(F32))
     stage_two = share_strips(1, stage_two)
-    build(bufd, lambda r: dh[r].astype(F32))
     convolve(bufd, 2, back)
     halo_d()
     edge_terms(3, 2)
@@ -490,7 +528,7 @@
         back[r] = dpre
         return sum_plain + fold(dpre), sum_cross + fold(dpre * normed)
 
-    sum_plain, sum_cross = lax.fori_loop(0, slots, slope_one, (zero8, zero8))
+    sum_plain, sum_cross = lax.fori_loop(0, slots, slope_one, (zero8, zero8), unroll=2)
     sums1 = send_block(3, by_row([flat(sum_plain), flat(sum_cross)]))
     stage_one = share_strips(0, stage_one)
     finish_grad(1, stage_two, grad2_ref)
@@ -531,6 +569,15 @@
         total = total + nbuf[i]
     norm_ref[...] = total[0:4]
     finish_grad(0, stage_one, grad1_ref)
+
+
+def place(*refs):
+    sems = refs[-1]
+    copies = [pltpu.make_async_copy(refs[k], refs[4 + k], sems.at[k]) for k in range(4)]
+    for copy in copies:
+        copy.start()
+    for copy in copies:
+        copy.wait()
 
 
 def body(
@@ -549,8 +596,15 @@
     _, slots, cols, chans = image_in.shape
     rows_out = 9 * chans // m
     vmem = pl.BlockSpec(memory_space=pltpu.VMEM)
+    hbm = pl.BlockSpec(memory_space=pltpu.HBM)
     padded = slots + 2
     scratch = [
+        pltpu.VMEM(image_in.shape, BF16),
+        pltpu.VMEM(cotangent.shape, BF16),
+        pltpu.VMEM(conv1_w.shape, BF16),
+        pltpu.VMEM(conv2_w.shape, BF16),
+        pltpu.VMEM((4, 1, chans), F32),
+        pltpu.SemaphoreType.DMA((CHUNKS + 7,)),
         pltpu.VMEM((padded, cols, 3 * chans), BF16),
         pltpu.VMEM((padded, cols, 3 * chans), BF16),
         pltpu.VMEM((padded, cols, 3 * chans), BF16),
@@ -581,7 +635,7 @@
         pltpu.SemaphoreType.DMA((2, n - 1)),
         pltpu.SemaphoreType.DMA((2, n - 1)),
     ]
-    return pl.pallas_call(
+    results = pl.pallas_call(
         functools.partial(kernel, n, m, rows_out),
         out_shape=(
             jax.ShapeDtypeStruct(image_in.shape, BF16),
@@ -589,7 +643,7 @@
             jax.ShapeDtypeStruct((rows_out, chans), F32),
             jax.ShapeDtypeStruct((4, chans), F32),
         ),
-        in_specs=[pl.BlockSpec(memory_space=pltpu.SMEM)] + [vmem] * 8,
+        in_specs=[pl.BlockSpec(memory_space=pltpu.SMEM)] + [hbm] * 8,
         out_specs=(vmem,) * 4,
         scratch_shapes=scratch,
         compiler_params=pltpu.CompilerParams(
@@ -597,15 +651,23 @@
         ),
     )(
         strip_rows,
-        image_in,
-        cotangent,
-        conv1_w,
-        conv2_w,
-        norm1_gain.reshape(1, chans),
-        norm1_shift.reshape(1, chans),
-        norm2_gain.reshape(1, chans),
-        norm2_shift.reshape(1, chans),
+        pltpu.with_memory_space_constraint(image_in, pltpu.HBM),
+        pltpu.with_memory_space_constraint(cotangent, pltpu.HBM),
+        pltpu.with_memory_space_constraint(conv1_w, pltpu.HBM),
+        pltpu.with_memory_space_constraint(conv2_w, pltpu.HBM),
+        pltpu.with_memory_space_constraint(norm1_gain.reshape(1, chans), pltpu.HBM),
+        pltpu.with_memory_space_constraint(norm1_shift.reshape(1, chans), pltpu.HBM),
+        pltpu.with_memory_space_constraint(norm2_gain.reshape(1, chans), pltpu.HBM),
+        pltpu.with_memory_space_constraint(norm2_shift.reshape(1, chans), pltpu.HBM),
     )
+    return pl.pallas_call(
+        place,
+        out_shape=tuple(jax.ShapeDtypeStruct(r.shape, r.dtype) for r in results),
+        in_specs=[vmem] * 4,
+        out_specs=(hbm,) * 4,
+        scratch_shapes=[pltpu.SemaphoreType.DMA((4,))],
+        compiler_params=pltpu.CompilerParams(vmem_limit_bytes=4 * 1024 * 1024),
+    )(*results)
 
 
 def solution(mesh):

time: 49.7 us -> 43.3 us (0.87)
  local copies, waits for them, and re-layouts: 7.86 us -> 0 us
  Pallas kernels: 40.3 us -> 41.9 us
    unnamed x20 -> x0, local copies, waits for them, and re-layouts: 7.86 us -> none
    pallas_call x0 -> x1, Pallas kernels: none -> 1.04 us  [body(): pl.pallas_call(place, out_shape=tuple((jax.ShapeDtypeStruct(r.shape, r.dt...]
    pallas_call x1, Pallas kernels: 40.3 us -> 40.8 us  [body(): pl.pallas_call(functools.partial(kernel, n, m, rows_out), out_shape=(jax....]
where the time goes in v2:
time: 43.3 us; the launch traced here: 43.2 us
  Pallas kernels  41.9 us (97%)
  between operations  1.29 us (3%)
    pallas_call x1, Pallas kernels, body(): pl.pallas_call(functools.partial(kernel, n, m, rows_out), out_shape=(jax....  40.8 us
    pallas_call x1, Pallas kernels, body(): pl.pallas_call(place, out_shape=tuple((jax.ShapeDtypeStruct(r.shape, r.dt...  1.04 us

profile of v2, /device:TPU:0, one launch (start us, length us, event | category | flops | bytes accessed | tf_op | source)
XLA Modules:
  0.0 43.2 jit_solution(16284106370936951563)
XLA Ops:
  1.3 40.8 %shard_map.120 = (bf16[1,32,128,128]{3,2,1,0:T(8,128)(2,1)S(1)}, f32[144,128]{1,0:T(8,128)S(1)}, f32[144,128]{1,0:T(8,128)S(1)}, f32[4,128]{1,0:T(4,128)S(1)}) custom-call(s32[1,1]{1,0:T(1,128)S(6)} %copy.13.len_ref, bf16[1,32,128,128]{3,2,1,0:T(8,128)(2,1)} %x_hbm.1, bf16[1,32,128,128]{3,2,1,0:T(8,128)(2,1)} %g_hbm.1, bf16[3,3,128,128]{3,2,1,0:T(8,128)(2,1)} %w1_hbm.1, ...), custom_call_target="tpu_custom_call" | custom-call | tf_op jit(solution)/shard_map/pallas_call | solution.py:638
  42.1 1.0 %shard_map.121 = (bf16[1,32,128,128]{3,2,1,0:T(8,128)(2,1)}, f32[144,128]{1,0:T(8,128)}, f32[144,128]{1,0:T(8,128)}, f32[4,128]{1,0:T(4,128)}) custom-call(bf16[1,32,128,128]{3,2,1,0:T(8,128)(2,1)S(1)} %get-tuple-element.8.refs_0_, f32[144,128]{1,0:T(8,128)S(1)} %get-tuple-element.9.refs_1_, f32[144,128]{1,0:T(8,128)S(1)} %get-tuple-element.10.refs_2_, ...), custom_call_target="tpu_custom_call" | custom-call | tf_op jit(solution)/shard_map/pallas_call | solution.py:663
